TPU v7x, 256 devices: a whole 4x4x8 slice. The times are simulated.
256 devices in a mesh: tile: 64 (over z, y_hi, x), sub: 4 (over y_lo, core).
Axes of the slice: x: 4, y: 4 (y_hi: 2, y_lo: 2; y = y_hi * 2 + y_lo), z: 8, core: 2. Of those that a mesh axis runs over, the one named last changes fastest.
Arguments:
- grid_feats: bfloat16 [32768, 512], P(('tile', 'sub')), may hold values from -6 to 6
- mesh_feats: bfloat16 [32768, 512], P(('tile', 'sub')), may hold values from -6 to 6
- encode_edges: bfloat16 [262144, 512], P(('tile', 'sub')), may hold values from -6 to 6
- decode_edges: bfloat16 [131072, 512], P(('tile', 'sub')), may hold values from -6 to 6
- encode_source: int32 [262144], P(('tile', 'sub')), may hold values from 0 to 32767, as said below
- encode_target: int32 [262144], P(('tile', 'sub')), may hold values from -1 to 32767, as said below
- decode_source: int32 [131072], P(('tile', 'sub')), may hold values from 0 to 32767, as said below
- decode_target: int32 [131072], P(('tile', 'sub')), may hold values from -1 to 32767, as said below
- owner_fine: int32 [32768], P(('tile', 'sub')), may hold values from 0 to 8191, as said below
- owner_coarse: int32 [8192], P('tile'), may hold values from 0 to 511
- encode_weight: bfloat16 [512, 512], replicated, may hold values from -0.25 to 0.25
- decode_weight: bfloat16 [512, 512], replicated, may hold values from -0.25 to 0.25
- middle_weight: bfloat16 [512, 512], replicated, may hold values from -0.25 to 0.25
- summit_weight: bfloat16 [512, 512], replicated, may hold values from -0.25 to 0.25
- cotangent: bfloat16 [32768, 512], P(('tile', 'sub')), may hold values from -6 to 6
Outputs:
- grid_update: bfloat16 [32768, 512], P(('tile', 'sub'))
- encode_grad: float32 [512, 512], replicated
- decode_grad: float32 [512, 512], replicated
- middle_grad: float32 [512, 512], replicated
- summit_grad: float32 [512, 512], replicated
Inputs may be any that keep to these rules, and one draw needn't show every extreme that they name: `encode_source`: edge slot e is listed on device d = e // 1024; its source grid node lies on device d - 1, d or d + 1. `encode_target`: -1 marks padding; every other value is a mesh node of the device that lists the slot. On each device padding fills whole blocks of 128 slots after all live ones; every device has a live block, and some device has no padding. `decode_source`: edge slot e is listed on device d = e // 512; its source mesh node lies on device d - 1, d or d + 1. `decode_target`: -1 marks padding; every other value is a grid node of the device that lists the slot. On each device padding fills whole blocks of 128 slots after all live ones; every device has a live block, and some device has no padding. `owner_fine`: the middle node of fine mesh node m lies on the tile of the device that holds m.
All inputs are finite; a program needn't handle non-finite values.
Results may differ from a plain program's by a relative error of at most 0.012.
Values may be sent and summed in bfloat16 or wider, within the bound.
A program may use at most 64 MiB of HBM per device.

v0:
```python
import jax
import jax.numpy as jnp
from jax import lax
from jax.sharding import PartitionSpec as P

TOP_NODES = 512
BLOCK = 128


def with_halo(x, sides, width):
    edges = {}
    for axis, dim in sides:
        peers, length = (lax.axis_size(axis), x.shape[dim])
        up = [(i, (i + 1) % peers) for i in range(peers - 1)]
        last = lax.slice_in_dim(x, length - width, length, axis=dim)
        initial = lax.slice_in_dim(x, 0, width, axis=dim)
        edges[dim] = (
            lax.ppermute(last, axis, up),
            lax.ppermute(initial, axis, [(b, a) for a, b in up]),
        )
    done = []
    for _, dim in sides:
        low, high = edges[dim]
        around = [(width, width) if d in done else (0, 0) for d in range(x.ndim)]
        x = jnp.concatenate([jnp.pad(low, around), x, jnp.pad(high, around)], axis=dim)
        done.append(dim)
    return x


def copy_for_each(x, axis):
    peers = lax.axis_size(axis)
    return lax.all_to_all(jnp.broadcast_to(x[None], (peers, *x.shape)), axis, 0, 0, tiled=True)


def taken_together(x, axis):
    return copy_for_each(x, axis).sum(axis=0)


def split_up(x, dim, peers):
    dims = x.shape
    pieces = x.reshape(*dims[:dim], peers, dims[dim] // peers, *dims[dim + 1 :])
    return jnp.moveaxis(pieces, dim, 0)


def summed_on_arrival(x, axis, dim):
    pieces = split_up(x, dim, lax.axis_size(axis))
    arrived = lax.all_to_all(pieces, axis, split_axis=0, concat_axis=0, tiled=True)
    return arrived.sum(axis=0)


def joined_along(pieces, dim):
    dims = list(pieces.shape[1:])
    dims[dim] *= pieces.shape[0]
    return jnp.moveaxis(pieces, 0, dim).reshape(dims)


def gather_directly(x, axis, dim):
    return joined_along(copy_for_each(x, axis), dim)


def from_behind(x, axis, by):
    peers = lax.axis_size(axis)
    pairs = [(i, i + by) for i in range(peers) if 0 <= i + by < peers]
    return lax.ppermute(x, axis, pairs)


def silu_slope(values):
    sigmoid = jax.nn.sigmoid(values)
    return sigmoid * (1.0 + values * (1.0 - sigmoid))


def live_count(targets):
    heads = targets.reshape(-1, BLOCK)[:, 0]
    return jnp.sum((heads >= 0).astype(jnp.int32))


def local_targets(targets, first, limit):
    return jnp.where(targets >= 0, targets - first, limit)


def outer_sum(left, right):
    return lax.dot_general(
        left, right, (((0,), (0,)), ((), ())), preferred_element_type=jnp.float32
    )


def times_transposed(left, right):
    return lax.dot_general(
        left, right, (((1,), (1,)), ((), ())), preferred_element_type=jnp.float32
    )


def membership(indices, rows, dtype):
    return (jnp.arange(rows, dtype=jnp.int32)[:, None] == indices[None, :]).astype(dtype)


def exact_sum(members, values):
    return jnp.dot(
        members, values, precision=lax.Precision.HIGHEST, preferred_element_type=jnp.float32
    )


def edge_forward(sources, senders, targets, edge_feats, weight, segments, blocks):
    features = weight.shape[1]

    def block_step(block_id, carried):
        summed, stored = carried
        offset = block_id * BLOCK
        picked = lax.dynamic_slice_in_dim(senders, offset, BLOCK)
        receivers = lax.dynamic_slice_in_dim(targets, offset, BLOCK)
        edge_part = lax.dynamic_slice_in_dim(edge_feats, offset, BLOCK, 0)
        fetched = jnp.take(sources, picked, axis=0)
        preact = jnp.dot(fetched, weight, preferred_element_type=jnp.float32) + edge_part.astype(
            jnp.float32
        )
        summed = summed + exact_sum(
            membership(receivers, segments, jnp.float32), jax.nn.silu(preact)
        )
        stored = lax.dynamic_update_slice_in_dim(stored, preact, offset, 0)
        return (summed, stored)

    start_sum = jnp.zeros((segments, features), jnp.float32)
    start_store = jnp.zeros((senders.shape[0], features), jnp.float32)
    return lax.fori_loop(0, blocks, block_step, (start_sum, start_store))


def edge_backward(
    sources, senders, targets, stored, weight, upstream, factor, blocks, returned_rows
):
    features = weight.shape[1]

    def block_step(block_id, carried):
        gradient, returned = carried
        offset = block_id * BLOCK
        picked = lax.dynamic_slice_in_dim(senders, offset, BLOCK)
        receivers = lax.dynamic_slice_in_dim(targets, offset, BLOCK)
        preact = lax.dynamic_slice_in_dim(stored, offset, BLOCK, 0)
        fetched = jnp.take(sources, picked, axis=0)
        incoming = jnp.take(upstream, receivers, axis=0).astype(jnp.float32) * factor
        slope = (incoming * silu_slope(preact)).astype(jnp.bfloat16)
        gradient = gradient + outer_sum(fetched, slope)
        if returned_rows:
            passed = times_transposed(slope, weight)
            returned = returned + exact_sum(membership(picked, returned_rows, jnp.float32), passed)
        return (gradient, returned)

    start_grad = jnp.zeros((features, features), jnp.float32)
    start_back = jnp.zeros((max(returned_rows, 1), features), jnp.float32)
    return lax.fori_loop(0, blocks, block_step, (start_grad, start_back))


def shards(
    grid_feats,
    mesh_feats,
    encode_edges,
    decode_edges,
    encode_source,
    encode_target,
    decode_source,
    decode_target,
    owner_fine,
    owner_coarse,
    encode_weight,
    decode_weight,
    middle_weight,
    summit_weight,
    cotangent,
):
    grid_rows = grid_feats.shape[0]
    mesh_rows = mesh_feats.shape[0]
    level_rows = owner_coarse.shape[0]
    tiles = lax.axis_size("tile")
    subs = lax.axis_size("sub")
    device = lax.axis_index(("tile", "sub"))
    tile_id = lax.axis_index("tile")
    encode_factor = mesh_rows / encode_source.shape[0]
    decode_factor = grid_rows / decode_source.shape[0]
    middle_factor = level_rows / (mesh_rows * subs)
    summit_factor = TOP_NODES / (level_rows * tiles)
    grid_wide = with_halo(grid_feats, ((("tile", "sub"), 0),), grid_rows)
    encode_senders = encode_source - (device - 1) * grid_rows
    encode_targets = local_targets(encode_target, device * mesh_rows, mesh_rows)
    encode_blocks = live_count(encode_target)
    encode_summed, encode_stored = edge_forward(
        grid_wide,
        encode_senders,
        encode_targets,
        encode_edges,
        encode_weight,
        mesh_rows,
        encode_blocks,
    )
    mesh_mid = (mesh_feats.astype(jnp.float32) + encode_factor * encode_summed).astype(jnp.bfloat16)
    fine_local = owner_fine - tile_id * level_rows
    fine_members = membership(fine_local, level_rows, jnp.bfloat16)
    middle_part = jnp.dot(fine_members, mesh_mid, preferred_element_type=jnp.float32)
    middle_sum = taken_together(middle_part, "sub")
    middle_in = (middle_factor * middle_sum).astype(jnp.bfloat16)
    middle_act = jnp.dot(middle_in, middle_weight, preferred_element_type=jnp.float32)
    middle_out = (middle_in.astype(jnp.float32) + jax.nn.silu(middle_act)).astype(jnp.bfloat16)
    top_members = membership(owner_coarse, TOP_NODES, jnp.bfloat16)
    summit_part = jnp.dot(top_members, middle_out, preferred_element_type=jnp.float32)
    summit_share = summed_on_arrival(summit_part, "tile", 0)
    summit_in = (summit_factor * summit_share).astype(jnp.bfloat16)
    summit_act = jnp.dot(summit_in, summit_weight, preferred_element_type=jnp.float32)
    summit_out = gather_directly(jax.nn.silu(summit_act).astype(jnp.bfloat16), "tile", 0)
    coarse_of = jnp.take(owner_coarse, fine_local)
    lifted = jnp.take(middle_out, fine_local, axis=0).astype(jnp.float32) + jnp.take(
        summit_out, coarse_of, axis=0
    ).astype(jnp.float32)
    mesh_out = (mesh_mid.astype(jnp.float32) + lifted).astype(jnp.bfloat16)
    mesh_wide = with_halo(mesh_out, ((("tile", "sub"), 0),), mesh_rows)
    decode_senders = decode_source - (device - 1) * mesh_rows
    decode_targets = local_targets(decode_target, device * grid_rows, grid_rows)
    decode_blocks = live_count(decode_target)
    decode_summed, decode_stored = edge_forward(
        mesh_wide,
        decode_senders,
        decode_targets,
        decode_edges,
        decode_weight,
        grid_rows,
        decode_blocks,
    )
    grid_update = (grid_feats.astype(jnp.float32) + decode_factor * decode_summed).astype(
        jnp.bfloat16
    )
    decode_local, decode_returned = edge_backward(
        mesh_wide,
        decode_senders,
        decode_targets,
        decode_stored,
        decode_weight,
        cotangent,
        decode_factor,
        decode_blocks,
        3 * mesh_rows,
    )
    from_next = from_behind(decode_returned[:mesh_rows], ("tile", "sub"), -1)
    from_prev = from_behind(decode_returned[2 * mesh_rows :], ("tile", "sub"), 1)
    mesh_grad = decode_returned[mesh_rows : 2 * mesh_rows] + from_next + from_prev
    level_part = exact_sum(fine_members.astype(jnp.float32), mesh_grad)
    level_grad = taken_together(level_part, "sub")
    summit_grad_part = exact_sum(top_members.astype(jnp.float32), level_grad)
    summit_grad_share = summed_on_arrival(summit_grad_part, "tile", 0)
    summit_slope = (summit_grad_share * silu_slope(summit_act)).astype(jnp.bfloat16)
    summit_local = outer_sum(summit_in, summit_slope)
    summit_back = gather_directly(
        times_transposed(summit_slope, summit_weight).astype(jnp.bfloat16), "tile", 0
    )
    level_total = level_grad + summit_factor * jnp.take(summit_back, owner_coarse, axis=0).astype(
        jnp.float32
    )
    middle_slope = (level_total * silu_slope(middle_act)).astype(jnp.bfloat16)
    middle_local = outer_sum(middle_in, middle_slope)
    middle_back = level_total + times_transposed(middle_slope, middle_weight)
    mesh_total = mesh_grad + middle_factor * jnp.take(middle_back, fine_local, axis=0)
    encode_local, unused_rows = edge_backward(
        grid_wide,
        encode_senders,
        encode_targets,
        encode_stored,
        encode_weight,
        mesh_total,
        encode_factor,
        encode_blocks,
        0,
    )
    sub_share = 1.0 / subs
    encode_grad, decode_grad, middle_grad, summit_grad = lax.psum(
        (encode_local, decode_local, sub_share * middle_local, sub_share * summit_local),
        ("tile", "sub"),
    )
    return (grid_update, encode_grad, decode_grad, middle_grad, summit_grad)


def solution(mesh):
    placed = (
        P(("tile", "sub"), None),
        P(("tile", "sub"), None),
        P(("tile", "sub"), None),
        P(("tile", "sub"), None),
        P(("tile", "sub")),
        P(("tile", "sub")),
        P(("tile", "sub")),
        P(("tile", "sub")),
        P(("tile", "sub")),
        P("tile"),
        P(),
        P(),
        P(),
        P(),
        P(("tile", "sub"), None),
    )
    return jax.shard_map(
        shards,
        mesh=mesh,
        in_specs=placed,
        out_specs=(P(("tile", "sub"), None), P(), P(), P(), P()),
        check_vma=False,
    )
```

profile of v0, /device:TPU:2, one launch (start us, length us, event | category | flops | bytes accessed | tf_op | source)
XLA Modules:
  0.0 638.4 jit_solution(1157762285381149726)
XLA Ops:
  7.2 2.1 collective-permute-start
  9.3 4.5 collective-permute-start.1
  15.2 1.4 convert_reduce_fusion
  16.6 0.9 constant_dynamic-update-slice_fusion.3
  17.5 1.6 broadcast_in_dim.117
  19.2 4.6 while.46
  20.8 1.9 constant_dynamic-update-slice_fusion.7
  24.2 41.1 %all_to_all.30 = f32[4,128,512]{2,1,0:T(8,128)S(1)} all-to-all(f32[4,128,512]{2,1,0:T(8,128)S(1)} %broadcast_in_dim.120), channel_id=1, replica_groups=mesh['tile'=64,'sub'=4] {'sub'}, dimensions={0} | all-to-all | bytes 2097152 | tf_op jit(solution)/shard_map/all_to_all | solution.py:32
  65.5 1.0 add_convert_fusion.2
  66.7 48.6 %all_to_all.31 = f32[64,8,512]{2,1,0:T(8,128)S(1)} all-to-all(f32[64,8,512]{2,1,0:T(8,128)S(1)} %convolution_bitcast_fusion), channel_id=1, replica_groups=mesh['tile'=64,'sub'=4] {'tile'}, dimensions={0} | all-to-all | bytes 2097152 | tf_op jit(solution)/shard_map/all_to_all | solution.py:47
  117.0 7.7 %all-to-all-start.2 = ((bf16[64,8,512]{2,1,0:T(8,128)(2,1)}), bf16[64,8,512]{2,1,0:T(8,128)(2,1)S(1)}, u32[]{:S(2)}, u32[]{:S(2)}) async-start(bf16[64,8,512]{2,1,0:T(8,128)(2,1)} %broadcast_in_dim.123), calls=%async_computation.2 | async-start | bytes 1048576 | tf_op jit(solution)/shard_map/all_to_all | solution.py:32
  124.8 1.2 gather_fusion.7
  126.9 14.6 %all-to-all-done.2 = bf16[64,8,512]{2,1,0:T(8,128)(2,1)S(1)} async-done(((bf16[64,8,512]{2,1,0:T(8,128)(2,1)}), bf16[64,8,512]{2,1,0:T(8,128)(2,1)S(1)}, u32[]{:S(2)}, u32[]{:S(2)}) %all-to-all-start.2) | async-done | bytes 524320 | tf_op jit(solution)/shard_map/all_to_all | solution.py:32
  142.5 1.9 collective-permute-start.2
  144.4 4.5 collective-permute-start.3
  150.3 1.2 collective-permute-done.3
  152.4 25.7 %while.47 = (s32[]{:T(128)}, f32[128,512]{1,0:T(8,128)}, f32[512,512]{1,0:T(8,128)S(1)}, s32[]{:T(128)}, s32[512]{0:T(512)}, /*index=5*/s32[512]{0:T(512)}, bf16...) while((s32[]{:T(128)}, f32[128,512]{1,0:T(8,128)}, ...), condition=%wide.region_7.10_spmd, body=%wide.region_6.9_spmd.sunk | while | flops 168314624 | bytes 2367799 | solution.py:124
  154.7 1.2 constant_dynamic-update-slice_fusion.8
  156.7 2.0 convolution_add_fusion.14
  161.0 1.2 constant_dynamic-update-slice_fusion.8
  162.9 2.0 convolution_add_fusion.14
  167.2 1.2 constant_dynamic-update-slice_fusion.8
  169.2 2.0 convolution_add_fusion.14
  173.5 1.2 constant_dynamic-update-slice_fusion.8
  175.5 2.0 convolution_add_fusion.14
  178.1 1.0 copy-done.8
  179.3 29.3 %while.48 = (s32[]{:T(128)}, f32[512,512]{1,0:T(8,128)S(1)}, f32[384,512]{1,0:T(8,128)S(1)}, s32[]{:T(128)}, s32[512]{0:T(512)}, /*index=5*/bf16[384,512]{1,0:T(...) while((s32[]{:T(128)}, f32[512,512]{1,0:T(8,128)S(1)}, ...), condition=%wide.region_9.12_spmd, body=%wide.region_8.11_spmd.sunk | while | flops 438357888 | bytes 8272603 | solution.py:149
  180.0 1.4 compare_and_fusion.16
  183.1 1.5 convolution_add_fusion.15
  184.6 1.3 fusion.84
  187.2 1.4 compare_and_fusion.16
  190.2 1.5 convolution_add_fusion.15
  191.8 1.3 fusion.84
  194.3 1.4 compare_and_fusion.16
  197.4 1.5 convolution_add_fusion.15
  199.0 1.3 fusion.84
  201.5 1.4 compare_and_fusion.16
  204.6 1.5 convolution_add_fusion.15
  206.1 1.3 fusion.84
  208.7 1.9 collective-permute-start.4
  210.6 2.4 collective-permute-start.5
  213.1 1.5 collective-permute-done.4
  214.6 4.7 collective-permute-done.5
  219.9 0.9 fusion.48
  220.8 1.1 broadcast_in_dim.126
  221.9 4.3 all-to-all-start.3
  226.2 14.5 %all-to-all-done.3 = f32[4,128,512]{2,1,0:T(8,128)} async-done(((f32[4,128,512]{2,1,0:T(8,128)}), f32[4,128,512]{2,1,0:T(8,128)}, u32[]{:S(2)}, u32[]{:S(2)}) %all-to-all-start.3) | async-done | bytes 1048608 | tf_op jit(solution)/shard_map/all_to_all | solution.py:32
  240.7 1.3 reduce_sum.58
  242.7 46.5 %all_to_all.32 = f32[64,8,512]{2,1,0:T(8,128)S(1)} all-to-all(f32[64,8,512]{2,1,0:T(8,128)S(1)} %fusion.42), channel_id=1, replica_groups=mesh['tile'=64,'sub'=4] {'tile'}, dimensions={0} | all-to-all | bytes 2097152 | tf_op jit(solution)/shard_map/all_to_all | solution.py:47
  289.3 1.3 convolution_convert_fusion
  291.5 7.7 %all-to-all-start.5 = ((bf16[64,8,512]{2,1,0:T(8,128)(2,1)}), bf16[64,8,512]{2,1,0:T(8,128)(2,1)S(1)}, u32[]{:S(2)}, u32[]{:S(2)}) async-start(bf16[64,8,512]{2,1,0:T(8,128)(2,1)} %broadcast_in_dim.127), calls=%async_computation.5 | async-start | bytes 1048576 | tf_op jit(solution)/shard_map/all_to_all | solution.py:32
  299.3 1.3 convolution_multiply_fusion
  300.6 15.4 %all-to-all-done.5 = bf16[64,8,512]{2,1,0:T(8,128)(2,1)S(1)} async-done(((bf16[64,8,512]{2,1,0:T(8,128)(2,1)}), bf16[64,8,512]{2,1,0:T(8,128)(2,1)S(1)}, u32[]{:S(2)}, u32[]{:S(2)}) %all-to-all-start.5) | async-done | bytes 524320 | tf_op jit(solution)/shard_map/all_to_all | solution.py:32
  316.9 1.4 convolution_multiply_fusion.1
  318.3 1.3 convolution_add_fusion.7
  319.6 0.9 gather_fusion.8
  320.8 5.2 while.49
  323.8 1.5 convolution_add_fusion.17
  326.0 0.9 copy-done.4
  328.0 298.2 %all-reduce.3.cloned.1.call-done = (f32[512,512]{1,0:T(8,128)}, f32[512,512]{1,0:T(8,128)}, f32[512,512]{1,0:T(8,128)}, f32[512,512]{1,0:T(8,128)}) async-done(((f32[512,512]{1,0:T(8,128)}, f32[512,512]{1,0:T(8,128)}, f32[512,512]{1,0:T(8,128)}, f32[512,512]{1,0:T(8,128)}), (f32[512,512]{1,0:T(8,128)}, f32[512,512]{1,0:T(8,128)}, f32[512,512]{1,0:T(8,128)}, ...) | async-done | bytes 4194320 | tf_op jit(solution)/shard_map/psum | solution.py:270
  626.2 2.4 copy.69
  628.6 1.0 copy.70
  629.6 1.0 copy.71
  630.6 1.0 copy.72
  (165 shorter events, 35.3 us)
Async XLA Ops:
  7.2 58.3 %copy-start = (bf16[512,512]{1,0:T(8,128)(2,1)S(1)}, bf16[512,512]{1,0:T(8,128)(2,1)}, u32[]{:S(2)}) copy-start(bf16[512,512]{1,0:T(8,128)(2,1)} %param.39) | copy-start | bytes 1572868
  7.2 12.0 %copy-start.5 = (bf16[512,512]{1,0:T(8,128)(2,1)S(1)}, bf16[512,512]{1,0:T(8,128)(2,1)}, u32[]{:S(2)}) copy-start(bf16[512,512]{1,0:T(8,128)(2,1)} %param.37) | copy-start | bytes 1572868
  7.2 9.4 %collective-permute-start = (bf16[128,512]{1,0:T(8,128)(2,1)}, bf16[128,512]{1,0:T(8,128)(2,1)S(1)}, u32[]{:S(2)}, u32[]{:S(2)}) collective-permute-start(bf16[128,512]{1,0:T(8,128)(2,1)} %param.27), channel_id=1, source_target_pairs={{0,1},{1,2},{2,3},{3,4},{4,5},{5,6},{6,7},{7,8},{8,9},{9,10},{10,1... | collective-permute-start | bytes 393224 | tf_op jit(solution)/shard_map/ppermute | solution.py:18
  9.3 8.2 %collective-permute-start.1 = (bf16[128,512]{1,0:T(8,128)(2,1)}, bf16[128,512]{1,0:T(8,128)(2,1)S(1)}, u32[]{:S(2)}, u32[]{:S(2)}) collective-permute-start(bf16[128,512]{1,0:T(8,128)(2,1)} %param.27), channel_id=1, source_target_pairs={{1,0},{2,1},{3,2},{4,3},{5,4},{6,5},{7,6},{8,7},{9,8},{10,9},{11,1... | collective-permute-start | bytes 393224 | tf_op jit(solution)/shard_map/ppermute | solution.py:19
  15.2 110.8 %copy-start.28 = (s32[128]{0:T(128)}, s32[128]{0:T(128)S(1)}, u32[]{:S(2)}) copy-start(s32[128]{0:T(128)S(1)} %get-tuple-element.301) | copy-start | bytes 1540
  19.2 4.7 copy-start.19
  23.8 41.6 %copy-start.25 = (s32[1024]{0:T(1024)}, s32[1024]{0:T(1024)S(1)}, u32[]{:S(2)}) copy-start(s32[1024]{0:T(1024)S(1)} %get-tuple-element.774) | copy-start | bytes 12292
  23.8 41.6 %copy-start.26 = (s32[1024]{0:T(1024)}, s32[1024]{0:T(1024)S(1)}, u32[]{:S(2)}) copy-start(s32[1024]{0:T(1024)S(1)} %get-tuple-element.775) | copy-start | bytes 12292
  24.2 42.2 %copy-start.1 = (s32[128]{0:T(128)S(1)}, s32[128]{0:T(128)}, u32[]{:S(2)}) copy-start(s32[128]{0:T(128)} %param.36) | copy-start | bytes 1540
  65.4 1.0 copy-start.20
  66.4 49.0 %copy-start.9 = (bf16[512,512]{1,0:T(8,128)(2,1)S(1)}, bf16[512,512]{1,0:T(8,128)(2,1)}, u32[]{:S(2)}) copy-start(bf16[512,512]{1,0:T(8,128)(2,1)} %param.40) | copy-start | bytes 1572868
  115.4 1.6 copy-start.22
  117.0 24.5 %all-to-all-start.2 = ((bf16[64,8,512]{2,1,0:T(8,128)(2,1)}), bf16[64,8,512]{2,1,0:T(8,128)(2,1)S(1)}, u32[]{:S(2)}, u32[]{:S(2)}) async-start(bf16[64,8,512]{2,1,0:T(8,128)(2,1)} %broadcast_in_dim.123), calls=%async_computation.2 | async-start | bytes 1048576 | tf_op jit(solution)/shard_map/all_to_all | solution.py:32
  124.7 24.3 %copy-start.27 = (s32[512]{0:T(512)S(1)}, s32[512]{0:T(512)}, u32[]{:S(2)}) copy-start(s32[512]{0:T(512)} %param.34) | copy-start | bytes 6148
  124.7 24.3 %copy-start.32 = (s32[512]{0:T(512)S(1)}, s32[512]{0:T(512)}, u32[]{:S(2)}) copy-start(s32[512]{0:T(512)} %param.33) | copy-start | bytes 6148
  124.8 26.7 %copy-start.29 = (s32[1024]{0:T(1024)}, s32[1024]{0:T(1024)S(1)}, u32[]{:S(2)}) copy-start(s32[1024]{0:T(1024)S(1)} %pad_clamp_fusion.8) | copy-start | bytes 12292
  126.0 24.3 %copy-start.30 = (pred[128]{0:T(512)(128)(4,1)}, pred[128]{0:T(512)(128)(4,1)S(1)}, u32[]{:S(2)}) copy-start(pred[128]{0:T(512)(128)(4,1)S(1)} %get-tuple-element.299) | copy-start | bytes 388
  126.9 25.5 %copy-start.6 = (bf16[512,512]{1,0:T(8,128)(2,1)S(1)}, bf16[512,512]{1,0:T(8,128)(2,1)}, u32[]{:S(2)}) copy-start(bf16[512,512]{1,0:T(8,128)(2,1)} %param.38) | copy-start | bytes 1572868
  142.5 7.8 %collective-permute-start.2 = (bf16[128,512]{1,0:T(8,128)(2,1)S(1)}, bf16[128,512]{1,0:T(8,128)(2,1)S(1)}, u32[]{:S(2)}, u32[]{:S(2)}) collective-permute-start(bf16[128,512]{1,0:T(8,128)(2,1)S(1)} %add_convert_fusion.1), channel_id=1, source_target_pairs={{0,1},{1,2},{2,3},{3,4},{4,5},{5,6},{6,7},{7,8},{8,9},{9,10},{10,1... | collective-permute-start | bytes 393224 | tf_op jit(solution)/shard_map/ppermute | solution.py:18
  144.4 7.0 %collective-permute-start.3 = (bf16[128,512]{1,0:T(8,128)(2,1)S(1)}, bf16[128,512]{1,0:T(8,128)(2,1)S(1)}, u32[]{:S(2)}, u32[]{:S(2)}) collective-permute-start(bf16[128,512]{1,0:T(8,128)(2,1)S(1)} %add_convert_fusion.1), channel_id=1, source_target_pairs={{1,0},{2,1},{3,2},{4,3},{5,4},{6,5},{7,6},{8,7},{9,8},{10,9},{11,1... | collective-permute-start | bytes 393224 | tf_op jit(solution)/shard_map/ppermute | solution.py:19
  152.4 26.9 %copy-start.2 = (bf16[128,512]{1,0:T(8,128)(2,1)S(1)}, bf16[128,512]{1,0:T(8,128)(2,1)}, u32[]{:S(2)}) copy-start(bf16[128,512]{1,0:T(8,128)(2,1)} %param.41) | copy-start | bytes 393220
  178.1 1.0 copy-start.8
  183.1 1.5 copy-start.7
  190.2 1.5 copy-start.7
  197.4 1.5 copy-start.7
  204.6 1.5 copy-start.7
  208.7 13.3 %copy-start.3 = (f32[512,512]{1,0:T(8,128)}, f32[512,512]{1,0:T(8,128)S(1)}, u32[]{:S(2)}) copy-start(f32[512,512]{1,0:T(8,128)S(1)} %get-tuple-element.208) | copy-start | bytes 3145732
  208.7 5.8 collective-permute-start.4
  210.6 8.6 %collective-permute-start.5 = (f32[128,512]{1,0:T(8,128)S(1)}, f32[128,512]{1,0:T(8,128)S(1)}, u32[]{:S(2)}, u32[]{:S(2)}) collective-permute-start(f32[128,512]{1,0:T(8,128)S(1)} %get-tuple-element.311), channel_id=1, source_target_pairs={{0,1},{1,2},{2,3},{3,4},{4,5},{5,6},{6,7},{7,8},{8,9},{9,10},{10,1... | collective-permute-start | bytes 786440 | tf_op jit(solution)/shard_map/ppermute | solution.py:64
  214.6 7.4 %copy-start.13 = (f32[128,512]{1,0:T(8,128)}, f32[128,512]{1,0:T(8,128)S(1)}, u32[]{:S(2)}) copy-start(f32[128,512]{1,0:T(8,128)S(1)} %collective-permute-done.4) | copy-start | bytes 786436
  219.2 0.7 copy-start.15
  221.9 18.8 %all-to-all-start.3 = ((f32[4,128,512]{2,1,0:T(8,128)}), f32[4,128,512]{2,1,0:T(8,128)}, u32[]{:S(2)}, u32[]{:S(2)}) async-start(f32[4,128,512]{2,1,0:T(8,128)} %broadcast_in_dim.126), calls=%async_computation.3 | async-start | bytes 2097152 | tf_op jit(solution)/shard_map/all_to_all | solution.py:32
  242.0 47.2 %copy-start.24 = (f32[8,512]{1,0:T(8,128)S(1)}, f32[8,512]{1,0:T(8,128)}, u32[]{:S(2)}) copy-start(f32[8,512]{1,0:T(8,128)} %get-tuple-element.315) | copy-start | bytes 49156
  289.2 10.1 %copy-start.23 = (f32[8,512]{1,0:T(8,128)S(1)}, f32[8,512]{1,0:T(8,128)}, u32[]{:S(2)}) copy-start(f32[8,512]{1,0:T(8,128)} %copy-done.22) | copy-start | bytes 49156
  289.3 27.6 %copy-start.21 = (f32[128,512]{1,0:T(8,128)S(1)}, f32[128,512]{1,0:T(8,128)}, u32[]{:S(2)}) copy-start(f32[128,512]{1,0:T(8,128)} %copy-done.20) | copy-start | bytes 786436
  289.3 27.6 %copy-start.33 = (f32[128,512]{1,0:T(8,128)S(1)}, f32[128,512]{1,0:T(8,128)}, u32[]{:S(2)}) copy-start(f32[128,512]{1,0:T(8,128)} %get-tuple-element.313) | copy-start | bytes 786436
  291.5 24.5 %all-to-all-start.5 = ((bf16[64,8,512]{2,1,0:T(8,128)(2,1)}), bf16[64,8,512]{2,1,0:T(8,128)(2,1)S(1)}, u32[]{:S(2)}, u32[]{:S(2)}) async-start(bf16[64,8,512]{2,1,0:T(8,128)(2,1)} %broadcast_in_dim.127), calls=%async_computation.5 | async-start | bytes 1048576 | tf_op jit(solution)/shard_map/all_to_all | solution.py:32
  299.2 327.0 %all-reduce.3.cloned.1.call-start = ((), (), s32[]{:S(2)}) async-start(), calls=%async_computation.6 | async-start | bytes 8388608 | tf_op jit(solution)/shard_map/psum | solution.py:270
  318.3 2.2 copy-start.14
  318.3 2.2 copy-start.16
  318.3 2.2 copy-start.31
  326.0 1.0 copy-start.4
  326.0 1.1 copy-start.17
  326.0 1.3 copy-start.18
  626.2 2.4 copy-start.12
  626.2 3.4 copy-start.11
  628.6 1.9 copy-start.10
Sparse Core Ops, SparseCore 0:
  327.1 299.0 all-reduce.2
where the time goes:
time: 641 us; the launch traced here: 638 us
  waiting for transfers between devices  350 us (55%)
  blocking collectives  136 us (21%)
  matrix products  39.3 us (6%)
  starting transfers between devices  37.1 us (6%)
  local copies, waits for them, and re-layouts  35.5 us (6%)
  other arithmetic  16.1 us (3%)
  between operations  14.7 us (2%)
  loops' own time  9.42 us (1%)
    psum x1, waiting for transfers between devices, shards(): lax.psum((encode_local, decode_local, sub_share * middle_local, sub_share...  298 us
    all_to_all x2, blocking collectives, summed_on_arrival(): lax.all_to_all(pieces, axis, split_axis=0, concat_axis=0, tiled=True)  95.1 us
    all_to_all x3, waiting for transfers between devices, copy_for_each(): lax.all_to_all(jnp.broadcast_to(x[None], (peers, *x.shape)), axis, 0, 0,...  44.5 us
    all_to_all x1, blocking collectives, copy_for_each(): lax.all_to_all(jnp.broadcast_to(x[None], (peers, *x.shape)), axis, 0, 0,...  41.1 us
    all_to_all x3, starting transfers between devices, copy_for_each(): lax.all_to_all(jnp.broadcast_to(x[None], (peers, *x.shape)), axis, 0, 0,...  19.7 us
  transfers between devices with their start and end apart: 10, of which 7 were waited for; matrix products, arithmetic and copies ran while one was open for 1% of the time, Pallas kernels for 0%

commit v1 on v0

--- a/solution.py
+++ b/solution.py
@@ -166,6 +166,12 @@
     summit_weight,
     cotangent,
 ):
+
+    def save_samples(load):
+        for dev in ("tile", "sub"):
+            load = lax.psum(load, dev)
+        return load
+
     grid_rows = grid_feats.shape[0]
     mesh_rows = mesh_feats.shape[0]
     level_rows = owner_coarse.shape[0]
@@ -267,9 +273,8 @@
         0,
     )
     sub_share = 1.0 / subs
-    encode_grad, decode_grad, middle_grad, summit_grad = lax.psum(
-        (encode_local, decode_local, sub_share * middle_local, sub_share * summit_local),
-        ("tile", "sub"),
+    encode_grad, decode_grad, middle_grad, summit_grad = save_samples(
+        (encode_local, decode_local, sub_share * middle_local, sub_share * summit_local)
     )
     return (grid_update, encode_grad, decode_grad, middle_grad, summit_grad)
 

time: 641 us -> 1180 us (1.84)
  waiting for transfers between devices: 350 us -> 885 us
    psum x1 -> x2, waiting for transfers between devices: 298 us -> 833 us  [save_samples(): load = lax.psum(load, dev)]
  transfers between devices with their start and end apart: 10 -> 11, of which waited for: 7 -> 8; matrix products, arithmetic and copies ran while one was open for 1% -> 1% of each run, Pallas kernels for 0% -> 0%
where the time goes in v1:
time: 1180 us; the launch traced here: 1170 us
  waiting for transfers between devices  885 us (75%)
  blocking collectives  136 us (12%)
  matrix products  39.3 us (3%)
  starting transfers between devices  37.2 us (3%)
  local copies, waits for them, and re-layouts  36.1 us (3%)
  other arithmetic  15.9 us (1%)
  between operations  14.7 us (1%)
    psum x2, waiting for transfers between devices, save_samples(): load = lax.psum(load, dev)  833 us
    all_to_all x2, blocking collectives, summed_on_arrival(): lax.all_to_all(pieces, axis, split_axis=0, concat_axis=0, tiled=True)  95.1 us
    all_to_all x3, waiting for transfers between devices, copy_for_each(): lax.all_to_all(jnp.broadcast_to(x[None], (peers, *x.shape)), axis, 0, 0,...  44.5 us
    all_to_all x1, blocking collectives, copy_for_each(): lax.all_to_all(jnp.broadcast_to(x[None], (peers, *x.shape)), axis, 0, 0,...  41.2 us
  transfers between devices with their start and end apart: 11, of which 8 were waited for; matrix products, arithmetic and copies ran while one was open for 1% of the time, Pallas kernels for 0%

profile of v1, /device:TPU:2, one launch (start us, length us, event | category | flops | bytes accessed | tf_op | source)
XLA Modules:
  0.0 1173.2 jit_solution(12485432320474309441)
XLA Ops:
  7.2 2.1 collective-permute-start
  9.3 4.5 collective-permute-start.1
  15.2 1.3 convert_reduce_fusion
  17.5 1.6 broadcast_in_dim.117
  19.1 4.6 while.46
  20.8 1.9 constant_dynamic-update-slice_fusion.7
  24.1 41.2 %all_to_all.30 = f32[4,128,512]{2,1,0:T(8,128)S(1)} all-to-all(f32[4,128,512]{2,1,0:T(8,128)S(1)} %broadcast_in_dim.120), channel_id=1, replica_groups=mesh['tile'=64,'sub'=4] {'sub'}, dimensions={0} | all-to-all | bytes 2097152 | tf_op jit(solution)/shard_map/all_to_all | solution.py:32
  65.4 0.9 add_convert_fusion.2
  66.6 48.6 %all_to_all.31 = f32[64,8,512]{2,1,0:T(8,128)S(1)} all-to-all(f32[64,8,512]{2,1,0:T(8,128)S(1)} %convolution_bitcast_fusion), channel_id=1, replica_groups=mesh['tile'=64,'sub'=4] {'tile'}, dimensions={0} | all-to-all | bytes 2097152 | tf_op jit(solution)/shard_map/all_to_all | solution.py:47
  117.0 7.7 all-to-all-start.2
  124.7 1.2 gather_fusion.7
  126.9 14.6 %all-to-all-done.2 = bf16[64,8,512]{2,1,0:T(8,128)(2,1)S(1)} async-done(((bf16[64,8,512]{2,1,0:T(8,128)(2,1)}), bf16[64,8,512]{2,1,0:T(8,128)(2,1)S(1)}, u32[]{:S(2)}, u32[]{:S(2)}) %all-to-all-start.2) | async-done | bytes 524320 | tf_op jit(solution)/shard_map/all_to_all | solution.py:32
  142.5 1.9 collective-permute-start.2
  144.4 4.5 collective-permute-start.3
  150.2 1.2 collective-permute-done.3
  152.4 25.3 %while.47 = (s32[]{:T(128)}, f32[128,512]{1,0:T(8,128)}, f32[512,512]{1,0:T(8,128)S(1)}, s32[]{:T(128)}, s32[512]{0:T(512)}, /*index=5*/s32[512]{0:T(512)}, bf16...) while((s32[]{:T(128)}, f32[128,512]{1,0:T(8,128)}, ...), condition=%wide.region_7.10_spmd, body=%wide.region_6.9_spmd.sunk | while | flops 168314624 | bytes 2367799 | solution.py:124
  154.6 1.2 constant_dynamic-update-slice_fusion.8
  156.5 2.0 convolution_add_fusion.14
  160.8 1.2 constant_dynamic-update-slice_fusion.8
  162.7 2.0 convolution_add_fusion.14
  167.0 1.2 constant_dynamic-update-slice_fusion.8
  168.9 2.0 convolution_add_fusion.14
  173.1 1.2 constant_dynamic-update-slice_fusion.8
  175.1 2.0 convolution_add_fusion.14
  177.7 1.0 copy-done.8
  178.9 29.0 %while.48 = (s32[]{:T(128)}, f32[512,512]{1,0:T(8,128)S(1)}, f32[384,512]{1,0:T(8,128)S(1)}, s32[]{:T(128)}, s32[512]{0:T(512)}, /*index=5*/bf16[384,512]{1,0:T(...) while((s32[]{:T(128)}, f32[512,512]{1,0:T(8,128)S(1)}, ...), condition=%wide.region_9.12_spmd, body=%wide.region_8.11_spmd.sunk | while | flops 438357888 | bytes 8272603 | solution.py:149
  179.5 1.3 compare_and_fusion.16
  182.6 1.5 convolution_add_fusion.15
  184.1 1.3 fusion.84
  186.6 1.3 compare_and_fusion.16
  189.7 1.5 convolution_add_fusion.15
  191.2 1.3 fusion.84
  193.7 1.3 compare_and_fusion.16
  196.8 1.5 convolution_add_fusion.15
  198.3 1.3 fusion.84
  200.8 1.3 compare_and_fusion.16
  203.9 1.5 convolution_add_fusion.15
  205.4 1.3 fusion.84
  207.9 1.9 collective-permute-start.4
  209.8 2.4 collective-permute-start.5
  212.3 1.5 collective-permute-done.4
  213.8 4.7 collective-permute-done.5
  219.1 1.0 fusion.48
  220.1 1.1 broadcast_in_dim.126
  221.2 4.3 all-to-all-start.3
  225.5 14.5 %all-to-all-done.3 = f32[4,128,512]{2,1,0:T(8,128)} async-done(((f32[4,128,512]{2,1,0:T(8,128)}), f32[4,128,512]{2,1,0:T(8,128)}, u32[]{:S(2)}, u32[]{:S(2)}) %all-to-all-start.3) | async-done | bytes 1048608 | tf_op jit(solution)/shard_map/all_to_all | solution.py:32
  240.0 1.3 reduce_sum.58
  242.0 46.5 %all_to_all.32 = f32[64,8,512]{2,1,0:T(8,128)S(1)} all-to-all(f32[64,8,512]{2,1,0:T(8,128)S(1)} %fusion.42), channel_id=1, replica_groups=mesh['tile'=64,'sub'=4] {'tile'}, dimensions={0} | all-to-all | bytes 2097152 | tf_op jit(solution)/shard_map/all_to_all | solution.py:47
  288.6 1.3 convolution_convert_fusion
  290.8 7.7 all-to-all-start.5
  298.6 1.3 convolution_multiply_fusion
  299.9 15.4 %all-to-all-done.5 = bf16[64,8,512]{2,1,0:T(8,128)(2,1)S(1)} async-done(((bf16[64,8,512]{2,1,0:T(8,128)(2,1)}), bf16[64,8,512]{2,1,0:T(8,128)(2,1)S(1)}, u32[]{:S(2)}, u32[]{:S(2)}) %all-to-all-start.5) | async-done | bytes 524320 | tf_op jit(solution)/shard_map/all_to_all | solution.py:32
  316.2 1.4 convolution_multiply_fusion.1
  317.6 1.3 convolution_add_fusion.7
  320.0 5.2 while.49
  323.1 1.5 convolution_add_fusion.17
  325.2 1.0 copy-done.4
  326.3 736.9 %all-reduce.5.cloned.1.call-done = (f32[512,512]{1,0:T(8,128)}, f32[512,512]{1,0:T(8,128)}, f32[512,512]{1,0:T(8,128)}, f32[512,512]{1,0:T(8,128)}) async-done(((f32[512,512]{1,0:T(8,128)}, f32[512,512]{1,0:T(8,128)}, f32[512,512]{1,0:T(8,128)}, f32[512,512]{1,0:T(8,128)}), (f32[512,512]{1,0:T(8,128)}, f32[512,512]{1,0:T(8,128)}, f32[512,512]{1,0:T(8,128)}, ...) | async-done | bytes 4194320 | tf_op jit(solution)/shard_map/psum | solution.py:172
  1063.2 0.9 copy-done.17
  1064.8 96.2 %all-reduce.7.cloned.1.call-done = (f32[512,512]{1,0:T(8,128)}, f32[512,512]{1,0:T(8,128)}, f32[512,512]{1,0:T(8,128)}, f32[512,512]{1,0:T(8,128)}) async-done(((f32[512,512]{1,0:T(8,128)}, f32[512,512]{1,0:T(8,128)}, f32[512,512]{1,0:T(8,128)}, f32[512,512]{1,0:T(8,128)}), (f32[512,512]{1,0:T(8,128)}, f32[512,512]{1,0:T(8,128)}, f32[512,512]{1,0:T(8,128)}, ...) | async-done | bytes 4194320 | tf_op jit(solution)/shard_map/psum | solution.py:172
  1161.0 2.4 copy.73
  1163.5 1.0 copy.74
  1164.4 1.0 copy.75
  1165.4 1.0 copy.76
  (168 shorter events, 36.7 us)
Async XLA Ops:
  7.2 58.2 %copy-start = (bf16[512,512]{1,0:T(8,128)(2,1)S(1)}, bf16[512,512]{1,0:T(8,128)(2,1)}, u32[]{:S(2)}) copy-start(bf16[512,512]{1,0:T(8,128)(2,1)} %param.39) | copy-start | bytes 1572868
  7.2 11.9 %copy-start.5 = (bf16[512,512]{1,0:T(8,128)(2,1)S(1)}, bf16[512,512]{1,0:T(8,128)(2,1)}, u32[]{:S(2)}) copy-start(bf16[512,512]{1,0:T(8,128)(2,1)} %param.37) | copy-start | bytes 1572868
  7.2 9.3 collective-permute-start
  9.3 8.2 collective-permute-start.1
  15.2 110.8 %copy-start.28 = (s32[128]{0:T(128)}, s32[128]{0:T(128)S(1)}, u32[]{:S(2)}) copy-start(s32[128]{0:T(128)S(1)} %get-tuple-element.305) | copy-start | bytes 1540
  19.1 4.7 copy-start.19
  23.8 41.6 %copy-start.25 = (s32[1024]{0:T(1024)}, s32[1024]{0:T(1024)S(1)}, u32[]{:S(2)}) copy-start(s32[1024]{0:T(1024)S(1)} %get-tuple-element.796) | copy-start | bytes 12292
  23.8 41.6 %copy-start.26 = (s32[1024]{0:T(1024)}, s32[1024]{0:T(1024)S(1)}, u32[]{:S(2)}) copy-start(s32[1024]{0:T(1024)S(1)} %get-tuple-element.797) | copy-start | bytes 12292
  24.1 42.3 %copy-start.1 = (s32[128]{0:T(128)S(1)}, s32[128]{0:T(128)}, u32[]{:S(2)}) copy-start(s32[128]{0:T(128)} %param.36) | copy-start | bytes 1540
  65.4 1.0 copy-start.20
  66.4 49.0 %copy-start.9 = (bf16[512,512]{1,0:T(8,128)(2,1)S(1)}, bf16[512,512]{1,0:T(8,128)(2,1)}, u32[]{:S(2)}) copy-start(bf16[512,512]{1,0:T(8,128)(2,1)} %param.40) | copy-start | bytes 1572868
  115.3 1.6 copy-start.22
  117.0 24.5 %all-to-all-start.2 = ((bf16[64,8,512]{2,1,0:T(8,128)(2,1)}), bf16[64,8,512]{2,1,0:T(8,128)(2,1)S(1)}, u32[]{:S(2)}, u32[]{:S(2)}) async-start(bf16[64,8,512]{2,1,0:T(8,128)(2,1)} %broadcast_in_dim.123), calls=%async_computation.2 | async-start | bytes 1048576 | tf_op jit(solution)/shard_map/all_to_all | solution.py:32
  124.7 24.3 %copy-start.27 = (s32[512]{0:T(512)S(1)}, s32[512]{0:T(512)}, u32[]{:S(2)}) copy-start(s32[512]{0:T(512)} %param.34) | copy-start | bytes 6148
  124.7 24.3 %copy-start.32 = (s32[512]{0:T(512)S(1)}, s32[512]{0:T(512)}, u32[]{:S(2)}) copy-start(s32[512]{0:T(512)} %param.33) | copy-start | bytes 6148
  124.7 26.7 %copy-start.29 = (s32[1024]{0:T(1024)}, s32[1024]{0:T(1024)S(1)}, u32[]{:S(2)}) copy-start(s32[1024]{0:T(1024)S(1)} %pad_clamp_fusion.8) | copy-start | bytes 12292
  126.0 24.2 %copy-start.30 = (pred[128]{0:T(512)(128)(4,1)}, pred[128]{0:T(512)(128)(4,1)S(1)}, u32[]{:S(2)}) copy-start(pred[128]{0:T(512)(128)(4,1)S(1)} %get-tuple-element.303) | copy-start | bytes 388
  126.9 25.5 %copy-start.6 = (bf16[512,512]{1,0:T(8,128)(2,1)S(1)}, bf16[512,512]{1,0:T(8,128)(2,1)}, u32[]{:S(2)}) copy-start(bf16[512,512]{1,0:T(8,128)(2,1)} %param.38) | copy-start | bytes 1572868
  142.5 7.7 collective-permute-start.2
  144.4 7.0 collective-permute-start.3
  152.4 26.5 %copy-start.2 = (bf16[128,512]{1,0:T(8,128)(2,1)S(1)}, bf16[128,512]{1,0:T(8,128)(2,1)}, u32[]{:S(2)}) copy-start(bf16[128,512]{1,0:T(8,128)(2,1)} %param.41) | copy-start | bytes 393220
  177.7 1.0 copy-start.8
  182.5 1.5 copy-start.7
  189.6 1.5 copy-start.7
  196.7 1.5 copy-start.7
  203.8 1.5 copy-start.7
  207.9 13.3 %copy-start.3 = (f32[512,512]{1,0:T(8,128)}, f32[512,512]{1,0:T(8,128)S(1)}, u32[]{:S(2)}) copy-start(f32[512,512]{1,0:T(8,128)S(1)} %get-tuple-element.208) | copy-start | bytes 3145732
  207.9 5.8 collective-permute-start.4
  209.8 8.6 collective-permute-start.5
  213.8 7.5 copy-start.13
  218.4 0.7 copy-start.15
  221.2 18.8 %all-to-all-start.3 = ((f32[4,128,512]{2,1,0:T(8,128)}), f32[4,128,512]{2,1,0:T(8,128)}, u32[]{:S(2)}, u32[]{:S(2)}) async-start(f32[4,128,512]{2,1,0:T(8,128)} %broadcast_in_dim.126), calls=%async_computation.3 | async-start | bytes 2097152 | tf_op jit(solution)/shard_map/all_to_all | solution.py:32
  241.3 47.2 %copy-start.24 = (f32[8,512]{1,0:T(8,128)S(1)}, f32[8,512]{1,0:T(8,128)}, u32[]{:S(2)}) copy-start(f32[8,512]{1,0:T(8,128)} %get-tuple-element.319) | copy-start | bytes 49156
  288.4 10.1 copy-start.23
  288.6 27.6 %copy-start.21 = (f32[128,512]{1,0:T(8,128)S(1)}, f32[128,512]{1,0:T(8,128)}, u32[]{:S(2)}) copy-start(f32[128,512]{1,0:T(8,128)} %copy-done.20) | copy-start | bytes 786436
  288.6 27.6 %copy-start.33 = (f32[128,512]{1,0:T(8,128)S(1)}, f32[128,512]{1,0:T(8,128)}, u32[]{:S(2)}) copy-start(f32[128,512]{1,0:T(8,128)} %get-tuple-element.317) | copy-start | bytes 786436
  290.8 24.5 %all-to-all-start.5 = ((bf16[64,8,512]{2,1,0:T(8,128)(2,1)}), bf16[64,8,512]{2,1,0:T(8,128)(2,1)S(1)}, u32[]{:S(2)}, u32[]{:S(2)}) async-start(bf16[64,8,512]{2,1,0:T(8,128)(2,1)} %broadcast_in_dim.127), calls=%async_computation.5 | async-start | bytes 1048576 | tf_op jit(solution)/shard_map/all_to_all | solution.py:32
  298.5 764.6 %all-reduce.5.cloned.1.call-start = ((), (), s32[]{:S(2)}) async-start(), calls=%async_computation.6 | async-start | bytes 8388608 | tf_op jit(solution)/shard_map/psum | solution.py:172
  317.6 2.2 copy-start.14
  317.6 2.2 copy-start.16
  317.6 2.2 copy-start.31
  325.2 1.0 copy-start.4
  326.2 834.8 %all-reduce.7.cloned.1.call-start = ((), (), s32[]{:S(2)}) async-start(), calls=%async_computation.7 | async-start | bytes 8388608 | tf_op jit(solution)/shard_map/psum | solution.py:172
  1063.1 0.9 copy-start.17
  1063.2 1.0 copy-start.18
  1161.0 2.4 copy-start.12
  1161.0 3.4 copy-start.11
  1163.5 1.9 copy-start.10
Sparse Core Ops, SparseCore 0:
  326.3 736.7 all-reduce.4
  1066.0 94.9 all-reduce.6
